TPU v7x, 32 devices: a whole 2x2x4 slice. The times are simulated.
32 devices in a mesh: groups: 2 (over y), dp: 4 (over z), mp: 4 (over x, core).
Axes of the slice: x: 2, y: 2, z: 4, core: 2. Of those that a mesh axis runs over, the one named last changes fastest.
Arguments:
- hidden: bfloat16 [8, 8192], P(('groups', 'mp'), 'dp'), parts along dimension 0, may hold values from -530 to 530
- attention_gain: float32 [8192], P('dp'), may hold values from 0.25 to 1.75
- query_weight: bfloat16 [8192, 8192], P('dp', 'mp'), may hold values from -0.0625 to 0.0625
- key_projector: bfloat16 [8192, 1024], P('dp', 'mp'), may hold values from -0.0625 to 0.0625
- value_projector: bfloat16 [8192, 1024], P('dp', 'mp'), may hold values from -0.0625 to 0.0625
- out_weight: bfloat16 [8192, 8192], P('mp', 'dp'), may hold values from -0.1875 to 0.1875
- key_cache: bfloat16 [8, 8, 256, 128], P(('groups', 'dp'), 'mp'), parts along dimension 0, may hold values from -1230 to 1230
- earlier_value_cache: bfloat16 [8, 8, 256, 128], P(('groups', 'dp'), 'mp'), parts along dimension 0, may hold values from -6 to 6
- cached_length_per_row: int32 [8], P(('groups', 'dp')), parts along dimension 0, may hold values from 1 to 256
- final_gain: float32 [8192], replicated, may hold values from 0.25 to 1.75
- head_weight: bfloat16 [32000, 8192], P('dp', 'mp'), may hold values from -41 to 41
- draft_ids: int32 [8], P(('groups', 'mp')), parts along dimension 0, may hold values from 0 to 31999
Outputs:
- residual_out: bfloat16 [8, 8192], P(('groups', 'mp'), 'dp'), parts along dimension 0
- draft_logprob: float32 [8], P(('groups', 'mp')), parts along dimension 0
There are 2 independent parts, one for each index of `groups`. A program takes and returns all parts, laid end to end along the dimension named above; an argument that names none is the same for every part. Nothing has to cross between parts.
All inputs are finite; a program needn't handle non-finite values.
Results may differ from a plain program's by a relative error of at most 0.0035.
Values may be sent and summed in bfloat16 or wider, within the bound.
A program may use at most 128 MiB of HBM per device.

v0:
```python
import jax
import jax.numpy as jnp
from jax import lax
from jax.sharding import PartitionSpec as P

MODEL_WIDTH = 8192
EPSILON = 1e-05
THETA = 10000.0


def rotary_embedding(vectors, positions):
    half_dim = vectors.shape[-1] // 2
    frequency = THETA ** (-2.0 * jnp.arange(half_dim, dtype=jnp.float32) / vectors.shape[-1])
    angles = positions.astype(jnp.float32)[:, None, None] * frequency[None, None, :]
    cosine = jnp.cos(angles)
    sine_part = jnp.sin(angles)
    former = vectors[..., :half_dim]
    latter = vectors[..., half_dim:]
    return jnp.concatenate(
        [former * cosine - latter * sine_part, latter * cosine + former * sine_part], axis=-1
    )


def rms_normed(matrix, gain_row):
    wide_rows = matrix.astype(jnp.float32)
    mean_square = jnp.mean(wide_rows * wide_rows, axis=-1, keepdims=True)
    return (wide_rows * lax.rsqrt(mean_square + EPSILON) * gain_row).astype(jnp.bfloat16)


def shards(
    hidden,
    attention_gain,
    query_weight,
    key_projector,
    value_projector,
    out_weight,
    key_cache,
    earlier_value_cache,
    cached_length_per_row,
    final_gain,
    head_weight,
    draft_ids,
):
    sequences = key_cache.shape[0]
    local_pairs = key_cache.shape[1]
    head_size = key_cache.shape[3]
    query_cols = query_weight.shape[1]
    pair_cols = key_projector.shape[1]
    local_heads = query_cols // head_size
    group_size = local_heads // local_pairs
    hidden_wide = hidden.astype(jnp.float32)
    squares_in = lax.psum(jnp.sum(hidden_wide * hidden_wide, axis=1), "dp")
    normed = (
        hidden_wide * lax.rsqrt(squares_in / MODEL_WIDTH + EPSILON)[:, None] * attention_gain
    ).astype(jnp.bfloat16)
    all_rows = lax.all_gather(normed, "mp", axis=0, tiled=True)
    picked_rows = all_rows
    projected = lax.psum_scatter(
        jnp.concatenate(
            [
                jnp.dot(picked_rows, weight, preferred_element_type=jnp.float32)
                for weight in (query_weight, key_projector, value_projector)
            ],
            axis=1,
        ),
        "dp",
        scatter_dimension=0,
        tiled=True,
    )
    query_rows = rotary_embedding(
        projected[:, :query_cols].reshape(sequences, local_heads, head_size), cached_length_per_row
    ).astype(jnp.bfloat16)
    query_rows = query_rows.reshape(sequences, local_pairs, group_size, head_size)
    incoming_key = rotary_embedding(
        projected[:, query_cols : query_cols + pair_cols].reshape(
            sequences, local_pairs, head_size
        ),
        cached_length_per_row,
    ).astype(jnp.bfloat16)
    incoming_value = (
        projected[:, query_cols + pair_cols :]
        .reshape(sequences, local_pairs, head_size)
        .astype(jnp.bfloat16)
    )
    score_scale = head_size ** (-0.5)
    own_score = (
        jnp.einsum("bgrd,bgd->bgr", query_rows, incoming_key, preferred_element_type=jnp.float32)
        * score_scale
    )
    scores = (
        jnp.einsum("bgrd,bgtd->bgrt", query_rows, key_cache, preferred_element_type=jnp.float32)
        * score_scale
    )
    places = lax.broadcasted_iota(jnp.int32, scores.shape, 3)
    scores = jnp.where(places < cached_length_per_row[:, None, None, None], scores, -jnp.inf)
    highest = jnp.maximum(jnp.max(scores, axis=3), own_score)
    exponent = jnp.exp(scores - highest[..., None])
    denominator = jnp.sum(exponent, axis=3)
    numerator = jnp.einsum(
        "bgrt,bgtd->bgrd",
        exponent.astype(jnp.bfloat16),
        earlier_value_cache,
        preferred_element_type=jnp.float32,
    )
    own_exp = jnp.exp(own_score - highest)
    denominator = denominator + own_exp
    own_weight = lax.optimization_barrier(own_exp.astype(jnp.bfloat16)).astype(jnp.float32)
    numerator = (
        numerator + own_weight[..., None] * incoming_value.astype(jnp.float32)[:, :, None, :]
    )
    mixed_heads = (
        (numerator / denominator[..., None]).astype(jnp.bfloat16).reshape(sequences, query_cols)
    )
    gathered = lax.all_gather(mixed_heads, "dp", axis=0, tiled=True)
    picked_rows = gathered
    attention_out = lax.psum_scatter(
        jnp.dot(picked_rows, out_weight, preferred_element_type=jnp.float32),
        "mp",
        scatter_dimension=0,
        tiled=True,
    )
    residual_out = (hidden_wide + attention_out).astype(jnp.bfloat16)
    full_rows = lax.all_gather(residual_out, "dp", axis=1, tiled=True)
    full_rows = rms_normed(full_rows, final_gain)
    columns = lax.all_to_all(full_rows, "mp", split_axis=1, concat_axis=0, tiled=True)
    picked_rows = columns
    logits = lax.psum_scatter(
        jnp.einsum("bd,vd->bv", picked_rows, head_weight, preferred_element_type=jnp.float32),
        "mp",
        scatter_dimension=0,
        tiled=True,
    )
    vocab_first = lax.axis_index("dp") * head_weight.shape[0]
    local_peak = jnp.max(logits, axis=1)
    local_mass = jnp.sum(jnp.exp(logits - local_peak[:, None]), axis=1)
    matches = lax.broadcasted_iota(jnp.int32, logits.shape, 1) + vocab_first == draft_ids[:, None]
    target_logit = jnp.sum(jnp.where(matches, logits, 0.0), axis=1)
    overall_peak = lax.pmax(local_peak, "dp")
    total_mass, total_target = lax.psum(
        (local_mass * jnp.exp(local_peak - overall_peak), target_logit), "dp"
    )
    log_total = overall_peak + jnp.log(total_mass)
    return (residual_out, total_target - log_total)


def solution(mesh):
    in_specs = (
        P(("groups", "mp"), "dp"),
        P("dp"),
        P("dp", "mp"),
        P("dp", "mp"),
        P("dp", "mp"),
        P("mp", "dp"),
        P(("groups", "dp"), "mp", None, None),
        P(("groups", "dp"), "mp", None, None),
        P(("groups", "dp")),
        P(),
        P("dp", "mp"),
        P(("groups", "mp")),
    )
    out_specs = (P(("groups", "mp"), "dp"), P(("groups", "mp")))
    return jax.shard_map(shards, mesh=mesh, in_specs=in_specs, out_specs=out_specs, check_vma=False)
```

profile of v0, /device:TPU:0, one launch (start us, length us, event | category | flops | bytes accessed | tf_op | source)
XLA Modules:
  0.0 190.5 jit_solution(16684031391719572066)
XLA Ops:
  7.2 1.4 multiply_reduce_fusion.1
  8.6 14.1 %psum.21 = f32[1]{0:T(128)} all-reduce(f32[1]{0:T(128)} %bitcast.1), channel_id=1, replica_groups=mesh['groups'=2,'dp'=4,'mp'=4] {'dp'}, use_global_device_ids=true, to_apply=%region_1.0 | all-reduce | flops 1 | bytes 8 | tf_op jit(solution)/shard_map/psum | solution.py:52
  23.4 0.7 convert_bitcast_fusion
  24.1 5.2 %all-gather = bf16[4,1,2048]{2,1,0:T(2,128)(2,1)S(1)} all-gather(bf16[1,1,2048]{2,1,0:T(2,128)(2,1)S(1)} %convert_bitcast_fusion), channel_id=1, replica_groups=mesh['groups'=2,'dp'=4,'mp'=4] {'mp'}, dimensions={0}, use_global_device_ids=true | all-gather | bytes 20480 | tf_op jit(solution)/shard_map/all_gather | solution.py:56
  29.3 4.7 %fusion.16 = f32[4,2048]{1,0:T(4,128)S(1)} fusion(bf16[2048,2048]{1,0:T(8,128)(2,1)} %param.14, bf16[4,1,2048]{2,1,0:T(2,128)(2,1)S(1)} %all-gather), kind=kOutput, calls=%fused_computation.23 | convolution fusion | flops 33554432 | bytes 8437760 | tf_op jit(solution)/shard_map/dot_general | solution.py:61
  34.0 0.2 fusion.12
  34.3 0.3 fusion.14
  34.6 16.2 %all-reduce = f32[4,2560]{1,0:T(4,128)S(1)} all-reduce(f32[4,2560]{1,0:T(4,128)S(1)} %pad_maximum_fusion), channel_id=2, replica_groups=mesh['groups'=2,'dp'=4,'mp'=4] {'dp'}, use_global_device_ids=true, to_apply=%region_2.0.clone | all-reduce | flops 10240 | bytes 81920
  50.8 0.6 dynamic-slice
  51.4 0.7 constant_dynamic-slice_fusion
  52.1 0.7 dynamic-slice.7
  53.7 0.2 fusion.26
  53.9 0.3 fusion.38
  54.2 0.2 fusion.18
  54.4 0.7 fusion.25
  55.1 0.2 fusion.2
  55.3 13.1 %all-gather.1 = bf16[4,1,2048]{2,1,0:T(2,128)(2,1)S(1)} all-gather(bf16[1,1,2048]{2,1,0:T(2,128)(2,1)S(1)} %reshape.192), channel_id=1, replica_groups=mesh['groups'=2,'dp'=4,'mp'=4] {'dp'}, dimensions={0}, use_global_device_ids=true | all-gather | bytes 20480 | tf_op jit(solution)/shard_map/all_gather | solution.py:114
  68.5 4.6 %fusion.9 = f32[4,2048]{1,0:T(4,128)S(1)} fusion(bf16[2048,2048]{1,0:T(8,128)(2,1)} %param.17, bf16[4,1,2048]{2,1,0:T(2,128)(2,1)S(1)} %all-gather.1), kind=kOutput, calls=%fused_computation.16 | convolution fusion | flops 33554432 | bytes 8437760 | tf_op jit(solution)/shard_map/dot_general | solution.py:117
  73.0 10.3 %all-reduce.1 = f32[4,2048]{1,0:T(4,128)S(1)} all-reduce(f32[4,2048]{1,0:T(4,128)S(1)} %fusion.9), channel_id=3, replica_groups=mesh['groups'=2,'dp'=4,'mp'=4] {'mp'}, use_global_device_ids=true, to_apply=%region_5.6.clone | all-reduce | flops 8192 | bytes 65536
  83.3 0.6 dynamic-slice.2
  83.9 0.7 fusion.21
  84.6 13.1 %all_gather.11 = bf16[1,8192]{1,0:T(2,128)(2,1)S(1)} all-gather(bf16[1,2048]{1,0:T(2,128)(2,1)S(1)} %fusion.21), channel_id=1, replica_groups=mesh['groups'=2,'dp'=4,'mp'=4] {'dp'}, dimensions={1}, use_global_device_ids=true | all-gather | bytes 20480 | tf_op jit(solution)/shard_map/all_gather | solution.py:123
  97.7 0.7 multiply_reduce_fusion
  99.3 0.6 broadcast.94
  99.9 0.8 reduce.9
  100.7 6.6 %all_to_all.16 = bf16[4,2,1024]{2,1,0:T(2,128)(2,1)S(1)} all-to-all(bf16[4,2,1024]{2,1,0:T(2,128)(2,1)S(1)} %reshape.200), channel_id=1, replica_groups=mesh['groups'=2,'dp'=4,'mp'=4] {'mp'}, dimensions={0} | all-to-all | bytes 32768 | tf_op jit(solution)/shard_map/all_to_all | solution.py:125
  107.3 14.4 %fusion.6 = f32[4,8000]{1,0:T(4,128)} fusion(bf16[8000,2048]{1,0:T(8,128)(2,1)} %param.22, bf16[1,4,2048]{2,0,1:T(2,128)(2,1)S(1)} %bitcast.66), kind=kOutput, calls=%fused_computation.13 | convolution fusion | flops 131072000 | bytes 32912384 | tf_op jit(solution)/shard_map/bd,vd->bv/dot_general | solution.py:128
  122.3 29.9 %all-reduce.6.cloned.1.call-done = f32[4,8000]{1,0:T(4,128)} async-done(((f32[4,8000]{1,0:T(4,128)}), f32[4,8000]{1,0:T(4,128)}) %all-reduce.6.cloned.1.call-update) | async-done | bytes 128016
  152.2 2.3 %dynamic-slice_reduce_fusion = f32[]{:T(128)} fusion(f32[4,8000]{1,0:T(4,128)} %all-reduce.6.cloned.1.call-done, u32[]{:T(128)} %bitcast.28), kind=kLoop, calls=%fused_computation.39 | loop fusion | flops 7999 | bytes 32008 | tf_op jit(solution)/shard_map/reduce_max | solution.py:134
  154.5 12.3 %pmax.7 = f32[1]{0:T(128)} all-reduce(f32[1]{0:T(128)} %bitcast.24), channel_id=1, replica_groups=mesh['groups'=2,'dp'=4,'mp'=4] {'dp'}, use_global_device_ids=true, to_apply=%region_11.12 | all-reduce | flops 1 | bytes 8 | tf_op jit(solution)/shard_map/pmax | solution.py:138
  168.0 3.0 %exponential_reduce_fusion = (f32[]{:T(128)}, f32[]{:T(128)}) fusion(f32[]{:T(128)} %dynamic-slice_reduce_fusion, f32[4,8000]{1,0:T(4,128)} %all-reduce.6.cloned.1.call-done, u32[]{:T(128)} %bitcast.28, s32[]{:T(128)} %bitcast.64, s32[]{:T(128)S(6)} %mul.175), kind=kLoop, calls=%fused_computation.11 | loop fusion | flops 47998 | bytes 32024 | tf_op jit(solution)/shard_map/reduce_sum | solution.py:135
  171.7 8.9 %all-reduce.3 = (f32[1]{0:T(128)}, f32[1]{0:T(128)}) all-reduce(f32[1]{0:T(128)} %bitcast.23, f32[1]{0:T(128)S(6)} %mul.180), channel_id=1, replica_groups=mesh['groups'=2,'dp'=4,'mp'=4] {'dp'}, use_global_device_ids=true, to_apply=%region_9.10 | all-reduce | flops 2 | bytes 16 | tf_op jit(solution)/shard_map/psum | solution.py:139
  (32 shorter events, 0.5 us)
Async XLA Ops:
  7.2 26.9 %copy-start = (bf16[2048,256]{1,0:T(8,128)(2,1)S(1)}, bf16[2048,256]{1,0:T(8,128)(2,1)}, u32[]{:S(2)}) copy-start(bf16[2048,256]{1,0:T(8,128)(2,1)} %param.16) | copy-start | bytes 3145732
  7.2 145.0 %all-reduce.6.cloned.1.call-start = ((), (), s32[]{:S(2)}) async-start(), calls=%async_computation.1 | async-start | bytes 258048
  29.3 4.9 %copy-start.1 = (bf16[2048,256]{1,0:T(8,128)(2,1)S(1)}, bf16[2048,256]{1,0:T(8,128)(2,1)}, u32[]{:S(2)}) copy-start(bf16[2048,256]{1,0:T(8,128)(2,1)} %param.15) | copy-start | bytes 3145732
  29.3 21.5 %copy-start.8 = (u32[32]{0:T(128)S(1)}, u32[32]{0:T(128)}, u32[]{:S(2)}) copy-start(u32[32]{0:T(128)} %constant.41) | copy-start | bytes 388
  29.3 24.6 %copy-start.2 = (bf16[1,2,256,128]{3,2,1,0:T(8,128)(2,1)S(1)}, bf16[1,2,256,128]{3,2,1,0:T(8,128)(2,1)}, u32[]{:S(2)}) copy-start(bf16[1,2,256,128]{3,2,1,0:T(8,128)(2,1)} %param.18) | copy-start | bytes 393220
  29.3 25.8 %copy-start.6 = (bf16[1,2,256,128]{3,2,1,0:T(8,128)(2,1)S(1)}, bf16[1,2,256,128]{3,2,1,0:T(8,128)(2,1)}, u32[]{:S(2)}) copy-start(bf16[1,2,256,128]{3,2,1,0:T(8,128)(2,1)} %param.19) | copy-start | bytes 393220
  34.5 48.8 %copy-start.7 = (u32[32]{0:T(128)S(1)}, u32[32]{0:T(128)}, u32[]{:S(2)}) copy-start(u32[32]{0:T(128)} %constant.45) | copy-start | bytes 388
  34.5 49.4 %copy-start.3 = (bf16[1,2048]{1,0:T(2,128)(2,1)S(1)}, bf16[1,2048]{1,0:T(2,128)(2,1)}, u32[]{:S(2)}) copy-start(bf16[1,2048]{1,0:T(2,128)(2,1)} %param.12) | copy-start | bytes 12292
  34.5 64.7 %copy-start.4 = (f32[8192]{0:T(1024)S(1)}, f32[8192]{0:T(1024)}, u32[]{:S(2)}) copy-start(f32[8192]{0:T(1024)} %param.21) | copy-start | bytes 98308
  84.6 37.0 %copy-start.5 = (bf16[1,2048]{1,0:T(2,128)(2,1)}, bf16[1,2048]{1,0:T(2,128)(2,1)S(1)}, u32[]{:S(2)}) copy-start(bf16[1,2048]{1,0:T(2,128)(2,1)S(1)} %fusion.21) | copy-start | bytes 12292
Sparse Core Ops, SparseCore 0:
  121.8 30.3 all-reduce.5
where the time goes:
time: 191 us
  blocking collectives  99.8 us (52%)
  waiting for transfers between devices  29.9 us (16%)
  matrix products  24.8 us (13%)
  between operations  21.9 us (11%)
  other arithmetic  10.9 us (6%)
  local copies, waits for them, and re-layouts  3.24 us (2%)
    unnamed x2, waiting for transfers between devices  29.9 us
    unnamed x2, blocking collectives  26.5 us
    dot_general x1, matrix products, shards(): jnp.einsum('bd,vd->bv', picked_rows, head_weight, preferred_element_type=...  14.4 us
    psum x1, blocking collectives, shards(): squares_in = lax.psum(jnp.sum(hidden_wide * hidden_wide, axis=1), 'dp')  14.1 us
    all_gather x1, blocking collectives, shards(): full_rows = lax.all_gather(residual_out, 'dp', axis=1, tiled=True)  13.1 us
    all_gather x1, blocking collectives, shards(): gathered = lax.all_gather(mixed_heads, 'dp', axis=0, tiled=True)  13.1 us
    pmax x1, blocking collectives, shards(): overall_peak = lax.pmax(local_peak, 'dp')  12.3 us
    psum x1, blocking collectives, shards(): lax.psum((local_mass * jnp.exp(local_peak - overall_peak), target_logit),...  8.95 us
  transfers between devices with their start and end apart: 1, of which 1 were waited for; matrix products, arithmetic and copies ran while one was open for 0% of the time, Pallas kernels for 0%

commit v1 on v0

--- a/solution.py
+++ b/solution.py
@@ -120,7 +120,12 @@
         tiled=True,
     )
     residual_out = (hidden_wide + attention_out).astype(jnp.bfloat16)
-    full_rows = lax.all_gather(residual_out, "dp", axis=1, tiled=True)
+    ring = [residual_out]
+    for hop in range(3):
+        ring.append(lax.ppermute(ring[-1], "dp", [(dev, (dev + 1) % 4) for dev in range(4)]))
+    full_rows = jnp.roll(
+        jnp.concatenate(ring[::-1], axis=1), (lax.axis_index("dp") + 1) * ring[0].shape[1], axis=1
+    )
     full_rows = rms_normed(full_rows, final_gain)
     columns = lax.all_to_all(full_rows, "mp", split_axis=1, concat_axis=0, tiled=True)
     picked_rows = columns

time: 191 us -> 193 us (1.010)
  waiting for transfers between devices: 29.9 us -> 44.7 us
  blocking collectives: 99.8 us -> 86.7 us
    ppermute x0 -> x3, waiting for transfers between devices: none -> 16.2 us  [shards(): lax.ppermute(ring[-1], 'dp', [(dev, (dev + 1) % 4) for dev in range(4)])]
    all_gather x1 -> x0, blocking collectives: 13.1 us -> none  [shards(): full_rows = lax.all_gather(residual_out, 'dp', axis=1, tiled=True)]
  transfers between devices with their start and end apart: 1 -> 4, of which waited for: 1 -> 4; matrix products, arithmetic and copies ran while one was open for 0% -> 0% of each run, Pallas kernels for 0% -> 0%
where the time goes in v1:
time: 193 us
  blocking collectives  86.7 us (45%)
  waiting for transfers between devices  44.7 us (23%)
  matrix products  24.8 us (13%)
  between operations  22 us (11%)
  other arithmetic  10.9 us (6%)
  local copies, waits for them, and re-layouts  3.36 us (2%)
    unnamed x2, waiting for transfers between devices  28.5 us
    unnamed x2, blocking collectives  26.5 us
    ppermute x3, waiting for transfers between devices, shards(): lax.ppermute(ring[-1], 'dp', [(dev, (dev + 1) % 4) for dev in range(4)])  16.2 us
    dot_general x1, matrix products, shards(): jnp.einsum('bd,vd->bv', picked_rows, head_weight, preferred_element_type=...  14.4 us
    psum x1, blocking collectives, shards(): squares_in = lax.psum(jnp.sum(hidden_wide * hidden_wide, axis=1), 'dp')  14.1 us
    all_gather x1, blocking collectives, shards(): gathered = lax.all_gather(mixed_heads, 'dp', axis=0, tiled=True)  13.1 us
    pmax x1, blocking collectives, shards(): overall_peak = lax.pmax(local_peak, 'dp')  12.3 us
    psum x1, blocking collectives, shards(): lax.psum((local_mass * jnp.exp(local_peak - overall_peak), target_logit),...  8.95 us
  transfers between devices with their start and end apart: 4, of which 4 were waited for; matrix products, arithmetic and copies ran while one was open for 0% of the time, Pallas kernels for 0%

profile of v1, /device:TPU:0, one launch (start us, length us, event | category | flops | bytes accessed | tf_op | source)
XLA Modules:
  0.0 192.6 jit_solution(1920496729438574153)
XLA Ops:
  7.2 1.4 multiply_reduce_fusion.1
  8.6 14.1 %psum.21 = f32[1]{0:T(128)} all-reduce(f32[1]{0:T(128)} %bitcast.1), channel_id=1, replica_groups=mesh['groups'=2,'dp'=4,'mp'=4] {'dp'}, use_global_device_ids=true, to_apply=%region_1.0 | all-reduce | flops 1 | bytes 8 | tf_op jit(solution)/shard_map/psum | solution.py:52
  23.4 0.7 convert_bitcast_fusion
  24.1 5.2 %all-gather = bf16[4,1,2048]{2,1,0:T(2,128)(2,1)S(1)} all-gather(bf16[1,1,2048]{2,1,0:T(2,128)(2,1)S(1)} %convert_bitcast_fusion), channel_id=1, replica_groups=mesh['groups'=2,'dp'=4,'mp'=4] {'mp'}, dimensions={0}, use_global_device_ids=true | all-gather | bytes 20480 | tf_op jit(solution)/shard_map/all_gather | solution.py:56
  29.3 4.7 %fusion.16 = f32[4,2048]{1,0:T(4,128)S(1)} fusion(bf16[2048,2048]{1,0:T(8,128)(2,1)} %param.14, bf16[4,1,2048]{2,1,0:T(2,128)(2,1)S(1)} %all-gather), kind=kOutput, calls=%fused_computation.31 | convolution fusion | flops 33554432 | bytes 8437760 | tf_op jit(solution)/shard_map/dot_general | solution.py:61
  34.0 0.2 fusion.12
  34.3 0.3 fusion.14
  34.6 16.2 %all-reduce = f32[4,2560]{1,0:T(4,128)S(1)} all-reduce(f32[4,2560]{1,0:T(4,128)S(1)} %pad_maximum_fusion), channel_id=2, replica_groups=mesh['groups'=2,'dp'=4,'mp'=4] {'dp'}, use_global_device_ids=true, to_apply=%region_2.0.clone | all-reduce | flops 10240 | bytes 81920
  50.8 0.6 dynamic-slice
  51.4 0.7 constant_dynamic-slice_fusion
  52.1 0.7 dynamic-slice.7
  53.9 0.3 fusion.38
  54.4 0.7 fusion.25
  55.1 0.2 fusion.2
  55.3 13.1 %all-gather.1 = bf16[4,1,2048]{2,1,0:T(2,128)(2,1)S(1)} all-gather(bf16[1,1,2048]{2,1,0:T(2,128)(2,1)S(1)} %reshape.192), channel_id=1, replica_groups=mesh['groups'=2,'dp'=4,'mp'=4] {'dp'}, dimensions={0}, use_global_device_ids=true | all-gather | bytes 20480 | tf_op jit(solution)/shard_map/all_gather | solution.py:114
  68.5 4.6 %fusion.9 = f32[4,2048]{1,0:T(4,128)S(1)} fusion(bf16[2048,2048]{1,0:T(8,128)(2,1)} %param.17, bf16[4,1,2048]{2,1,0:T(2,128)(2,1)S(1)} %all-gather.1), kind=kOutput, calls=%fused_computation.24 | convolution fusion | flops 33554432 | bytes 8437760 | tf_op jit(solution)/shard_map/dot_general | solution.py:117
  73.0 10.3 %all-reduce.1 = f32[4,2048]{1,0:T(4,128)S(1)} all-reduce(f32[4,2048]{1,0:T(4,128)S(1)} %fusion.9), channel_id=3, replica_groups=mesh['groups'=2,'dp'=4,'mp'=4] {'mp'}, use_global_device_ids=true, to_apply=%region_5.6.clone | all-reduce | flops 8192 | bytes 65536
  83.3 0.6 dynamic-slice.2
  83.9 0.7 fusion.21
  84.8 5.3 %collective-permute-done = bf16[1,2048]{1,0:T(2,128)(2,1)S(1)} collective-permute-done((bf16[1,2048]{1,0:T(2,128)(2,1)S(1)}, bf16[1,2048]{1,0:T(2,128)(2,1)S(1)}, u32[]{:S(2)}, u32[]{:S(2)}) %collective-permute-start) | collective-permute-done | bytes 4128 | tf_op jit(solution)/shard_map/ppermute | solution.py:125
  90.1 5.4 %collective-permute-done.1 = bf16[1,2048]{1,0:T(2,128)(2,1)S(1)} collective-permute-done((bf16[1,2048]{1,0:T(2,128)(2,1)S(1)}, bf16[1,2048]{1,0:T(2,128)(2,1)S(1)}, u32[]{:S(2)}, u32[]{:S(2)}) %collective-permute-start.1) | collective-permute-done | bytes 4128 | tf_op jit(solution)/shard_map/ppermute | solution.py:125
  95.5 5.4 %collective-permute-done.2 = bf16[1,2048]{1,0:T(2,128)(2,1)S(1)} collective-permute-done((bf16[1,2048]{1,0:T(2,128)(2,1)S(1)}, bf16[1,2048]{1,0:T(2,128)(2,1)S(1)}, u32[]{:S(2)}, u32[]{:S(2)}) %collective-permute-start.2) | collective-permute-done | bytes 4128 | tf_op jit(solution)/shard_map/ppermute | solution.py:125
  101.2 0.8 multiply_reduce_fusion
  102.7 0.6 broadcast.95
  103.3 0.8 reduce.9
  104.1 6.6 %all_to_all.16 = bf16[4,2,1024]{2,1,0:T(2,128)(2,1)S(1)} all-to-all(bf16[4,2,1024]{2,1,0:T(2,128)(2,1)S(1)} %reshape.200), channel_id=1, replica_groups=mesh['groups'=2,'dp'=4,'mp'=4] {'mp'}, dimensions={0} | all-to-all | bytes 32768 | tf_op jit(solution)/shard_map/all_to_all | solution.py:130
  110.7 14.4 %fusion.6 = f32[4,8000]{1,0:T(4,128)} fusion(bf16[8000,2048]{1,0:T(8,128)(2,1)} %param.22, bf16[1,4,2048]{2,0,1:T(2,128)(2,1)S(1)} %bitcast.66), kind=kOutput, calls=%fused_computation.21 | convolution fusion | flops 131072000 | bytes 32912384 | tf_op jit(solution)/shard_map/bd,vd->bv/dot_general | solution.py:133
  125.7 28.5 %all-reduce.6.cloned.1.call-done = f32[4,8000]{1,0:T(4,128)} async-done(((f32[4,8000]{1,0:T(4,128)}), f32[4,8000]{1,0:T(4,128)}) %all-reduce.6.cloned.1.call-update) | async-done | bytes 128016
  154.2 2.3 %dynamic-slice_reduce_fusion = f32[]{:T(128)} fusion(f32[4,8000]{1,0:T(4,128)} %all-reduce.6.cloned.1.call-done, u32[]{:T(128)} %bitcast.28), kind=kLoop, calls=%fused_computation.47 | loop fusion | flops 7999 | bytes 32008 | tf_op jit(solution)/shard_map/reduce_max | solution.py:139
  156.5 12.3 %pmax.7 = f32[1]{0:T(128)} all-reduce(f32[1]{0:T(128)} %bitcast.24), channel_id=1, replica_groups=mesh['groups'=2,'dp'=4,'mp'=4] {'dp'}, use_global_device_ids=true, to_apply=%region_11.12 | all-reduce | flops 1 | bytes 8 | tf_op jit(solution)/shard_map/pmax | solution.py:143
  170.1 3.0 %exponential_reduce_fusion = (f32[]{:T(128)}, f32[]{:T(128)}) fusion(f32[]{:T(128)} %dynamic-slice_reduce_fusion, f32[4,8000]{1,0:T(4,128)} %all-reduce.6.cloned.1.call-done, u32[]{:T(128)} %bitcast.28, s32[]{:T(128)} %bitcast.64, s32[]{:T(128)S(6)} %mul.178), kind=kLoop, calls=%fused_computation.11 | loop fusion | flops 47998 | bytes 32024 | tf_op jit(solution)/shard_map/reduce_sum | solution.py:140
  173.7 8.9 %all-reduce.3 = (f32[1]{0:T(128)}, f32[1]{0:T(128)}) all-reduce(f32[1]{0:T(128)} %bitcast.23, f32[1]{0:T(128)S(6)} %mul.184), channel_id=1, replica_groups=mesh['groups'=2,'dp'=4,'mp'=4] {'dp'}, use_global_device_ids=true, to_apply=%region_9.10 | all-reduce | flops 2 | bytes 16 | tf_op jit(solution)/shard_map/psum | solution.py:144
  (45 shorter events, 1.2 us)
Async XLA Ops:
  7.2 26.9 %copy-start = (bf16[2048,256]{1,0:T(8,128)(2,1)S(1)}, bf16[2048,256]{1,0:T(8,128)(2,1)}, u32[]{:S(2)}) copy-start(bf16[2048,256]{1,0:T(8,128)(2,1)} %param.16) | copy-start | bytes 3145732
  7.2 147.0 %all-reduce.6.cloned.1.call-start = ((), (), s32[]{:S(2)}) async-start(), calls=%async_computation.1 | async-start | bytes 258048
  29.3 4.9 %copy-start.1 = (bf16[2048,256]{1,0:T(8,128)(2,1)S(1)}, bf16[2048,256]{1,0:T(8,128)(2,1)}, u32[]{:S(2)}) copy-start(bf16[2048,256]{1,0:T(8,128)(2,1)} %param.15) | copy-start | bytes 3145732
  29.3 21.5 %copy-start.8 = (u32[32]{0:T(128)S(1)}, u32[32]{0:T(128)}, u32[]{:S(2)}) copy-start(u32[32]{0:T(128)} %constant.67) | copy-start | bytes 388
  29.3 24.6 %copy-start.2 = (bf16[1,2,256,128]{3,2,1,0:T(8,128)(2,1)S(1)}, bf16[1,2,256,128]{3,2,1,0:T(8,128)(2,1)}, u32[]{:S(2)}) copy-start(bf16[1,2,256,128]{3,2,1,0:T(8,128)(2,1)} %param.18) | copy-start | bytes 393220
  29.3 25.8 %copy-start.6 = (bf16[1,2,256,128]{3,2,1,0:T(8,128)(2,1)S(1)}, bf16[1,2,256,128]{3,2,1,0:T(8,128)(2,1)}, u32[]{:S(2)}) copy-start(bf16[1,2,256,128]{3,2,1,0:T(8,128)(2,1)} %param.19) | copy-start | bytes 393220
  34.5 48.8 %copy-start.7 = (u32[32]{0:T(128)S(1)}, u32[32]{0:T(128)}, u32[]{:S(2)}) copy-start(u32[32]{0:T(128)} %constant.71) | copy-start | bytes 388
  34.5 49.4 %copy-start.3 = (bf16[1,2048]{1,0:T(2,128)(2,1)S(1)}, bf16[1,2048]{1,0:T(2,128)(2,1)}, u32[]{:S(2)}) copy-start(bf16[1,2048]{1,0:T(2,128)(2,1)} %param.12) | copy-start | bytes 12292
  34.5 68.1 %copy-start.5 = (f32[8192]{0:T(1024)S(1)}, f32[8192]{0:T(1024)}, u32[]{:S(2)}) copy-start(f32[8192]{0:T(1024)} %param.21) | copy-start | bytes 98308
  84.6 40.5 %copy-start.4 = (bf16[1,2048]{1,0:T(2,128)(2,1)}, bf16[1,2048]{1,0:T(2,128)(2,1)S(1)}, u32[]{:S(2)}) copy-start(bf16[1,2048]{1,0:T(2,128)(2,1)S(1)} %fusion.21) | copy-start | bytes 12292
  84.6 5.5 %collective-permute-start = (bf16[1,2048]{1,0:T(2,128)(2,1)S(1)}, bf16[1,2048]{1,0:T(2,128)(2,1)S(1)}, u32[]{:S(2)}, u32[]{:S(2)}) collective-permute-start(bf16[1,2048]{1,0:T(2,128)(2,1)S(1)} %fusion.21), channel_id=1, source_target_pairs={{0,4},{4,8},{8,12},{12,0},{1,5},{5,9},{9,13},{13,1},{2,6},{6,10},{... | collective-permute-start | bytes 12296 | tf_op jit(solution)/shard_map/ppermute | solution.py:125
  90.1 5.4 %collective-permute-start.1 = (bf16[1,2048]{1,0:T(2,128)(2,1)S(1)}, bf16[1,2048]{1,0:T(2,128)(2,1)S(1)}, u32[]{:S(2)}, u32[]{:S(2)}) collective-permute-start(bf16[1,2048]{1,0:T(2,128)(2,1)S(1)} %collective-permute-done), channel_id=1, source_target_pairs={{0,4},{4,8},{8,12},{12,0},{1,5},{5,9},{9,13},{13,1},{2,6},{6,10},{... | collective-permute-start | bytes 12296 | tf_op jit(solution)/shard_map/ppermute | solution.py:125
  95.5 5.4 %collective-permute-start.2 = (bf16[1,2048]{1,0:T(2,128)(2,1)S(1)}, bf16[1,2048]{1,0:T(2,128)(2,1)S(1)}, u32[]{:S(2)}, u32[]{:S(2)}) collective-permute-start(bf16[1,2048]{1,0:T(2,128)(2,1)S(1)} %collective-permute-done.1), channel_id=1, source_target_pairs={{0,4},{4,8},{8,12},{12,0},{1,5},{5,9},{9,13},{13,1},{2,6},{6,10},{... | collective-permute-start | bytes 12296 | tf_op jit(solution)/shard_map/ppermute | solution.py:125
Sparse Core Ops, SparseCore 0:
  125.2 28.9 all-reduce.5
